TPU v7x, 32 devices: a whole 2x2x4 slice. The times are simulated.
32 devices in a mesh: batch: 8 (over y, x, core), tensor: 4 (over z).
Axes of the slice: x: 2, y: 2, z: 4, core: 2. Of those that a mesh axis runs over, the one named last changes fastest.
Arguments:
- inputs: bfloat16 [8, 4096, 1024], P('batch'), may hold values from -6 to 6
- segments: int32 [8, 4096], P('batch'), may hold values from 0 to 7, never falling along the last dimension, each value on 1 to 2048 neighbouring positions
- valid: int32 [8, 4096], P('batch'), may hold values from 0 to 1, as said below
- w_query: bfloat16 [1024, 1024], P(None, 'tensor'), may hold values from -0.1875 to 0.1875
- b_query: bfloat16 [1024], P('tensor'), may hold values from -3 to 3
- w_key: bfloat16 [1024, 1024], P(None, 'tensor'), may hold values from -0.1875 to 0.1875
- w_value: bfloat16 [1024, 1024], P(None, 'tensor'), may hold values from -0.1875 to 0.1875
- b_value: bfloat16 [1024], P('tensor'), may hold values from -3 to 3
- w_out: bfloat16 [1024, 1024], P('tensor'), may hold values from -1.5 to 1.5
- b_out: bfloat16 [1024], P('tensor'), may hold values from -3 to 3
- gain_one: bfloat16 [1024], P('tensor'), may hold values from 0.25 to 1.75
- shift_one: bfloat16 [1024], P('tensor'), may hold values from -2 to 2
- w_up: bfloat16 [1024, 4096], P(None, 'tensor'), may hold values from -0.1875 to 0.1875
- b_up: bfloat16 [4096], P('tensor'), may hold values from -3 to 3
- w_down: bfloat16 [4096, 1024], P('tensor'), may hold values from -0.09375 to 0.09375
- b_down: bfloat16 [1024], P('tensor'), may hold values from -3 to 3
- gain_two: bfloat16 [1024], P('tensor'), may hold values from 0.25 to 1.75
- shift_two: bfloat16 [1024], P('tensor'), may hold values from -2 to 2
- lex_weight: bfloat16 [1024], P('tensor'), may hold values from -0.1875 to 0.1875
- lex_bias: bfloat16 [1], replicated, may hold values from -0.5 to 0.5
- cotangent: bfloat16 [8, 4096, 1024], P('batch', None, 'tensor'), may hold values from -6 to 6
Outputs:
- output: bfloat16 [8, 4096, 1024], P('batch', None, 'tensor')
- grad_inputs: bfloat16 [8, 4096, 1024], P('batch', None, 'tensor')
- grad_w_query: float32 [1024, 1024], P(None, 'tensor')
- grad_b_query: float32 [1024], P('tensor')
- grad_w_key: float32 [1024, 1024], P(None, 'tensor')
- grad_w_value: float32 [1024, 1024], P(None, 'tensor')
- grad_b_value: float32 [1024], P('tensor')
- grad_w_out: float32 [1024, 1024], P('tensor')
- grad_b_out: float32 [1024], P('tensor')
- grad_gain_one: float32 [1024], P('tensor')
- grad_shift_one: float32 [1024], P('tensor')
- grad_w_up: float32 [1024, 4096], P(None, 'tensor')
- grad_b_up: float32 [4096], P('tensor')
- grad_w_down: float32 [4096, 1024], P('tensor')
- grad_b_down: float32 [1024], P('tensor')
- grad_gain_two: float32 [1024], P('tensor')
- grad_shift_two: float32 [1024], P('tensor')
- lex_stats: float32 [2], replicated
Inputs may be any that keep to these rules, and one draw needn't show every extreme that they name: `valid`: in each row, 1 on a leading run of tokens and 0 on the rest (its padding); at least a quarter of each row is 1.
All inputs are finite; a program needn't handle non-finite values.
Results may differ from a plain program's by a relative error of at most 0.02.
Values may be sent and summed in bfloat16 or wider, within the bound.
A program may use at most 256 MiB of HBM per device.

v0:
```python
import math

import jax
import jax.numpy as jnp
from jax import lax
from jax.sharding import PartitionSpec as P

HEAD_DIM = 64


EPSILON = 1e-05
MASKED = -1e30


def inner_first(left, right):
    return lax.dot_general(
        left, right, (((0,), (0,)), ((), ())), preferred_element_type=jnp.float32
    )


def inner_last(left, right):
    return lax.dot_general(
        left, right, (((1,), (1,)), ((), ())), preferred_element_type=jnp.float32
    )


def gelu_exact(value):
    return 0.5 * value * (1.0 + lax.erf(value * (1.0 / math.sqrt(2.0))))


def norm_from_sums(first_sum, second_sum, full_width):
    mean_value = first_sum / full_width
    spread = second_sum / full_width - mean_value * mean_value
    return (mean_value, lax.rsqrt(spread + EPSILON))


def allowed_block(seg_row, valid_row, block_start, block_size):
    seg_query = lax.dynamic_slice_in_dim(seg_row, block_start, block_size, 0)
    query_pos = block_start + jnp.arange(block_size, dtype=jnp.int32)
    key_pos = jnp.arange(seg_row.shape[0], dtype=jnp.int32)
    same_text = (seg_query[:, None] == seg_row[None, :]) & (valid_row[None, :] == 1)
    return same_text | (query_pos[:, None] == key_pos[None, :])


def block_scores(query_block, key_rows, allowed, score_scale):
    scores = (
        jnp.einsum("qhd,khd->hqk", query_block, key_rows, preferred_element_type=jnp.float32)
        * score_scale
    )
    return jnp.where(allowed[None], scores, MASKED)


def attend_forward(row_items):
    queries, key_rows, value_rows, seg_row, valid_row = row_items
    seq_len = queries.shape[0]
    block_size = min(512, seq_len)
    score_scale = 1.0 / math.sqrt(HEAD_DIM)

    def one_block(block_index):
        block_start = block_index * block_size
        query_block = lax.dynamic_slice_in_dim(queries, block_start, block_size, 0)
        allowed = allowed_block(seg_row, valid_row, block_start, block_size)
        scores = block_scores(query_block, key_rows, allowed, score_scale)
        row_max = jnp.max(scores, axis=2, keepdims=True)
        expo = jnp.exp(scores - row_max)
        denom_sum = jnp.sum(expo, axis=2, keepdims=True)
        weights = (expo / denom_sum).astype(jnp.bfloat16)
        context = jnp.einsum(
            "hqk,khd->qhd", weights, value_rows, preferred_element_type=jnp.float32
        )
        return (context.astype(jnp.bfloat16), (row_max + jnp.log(denom_sum))[:, :, 0])

    contexts, log_sums = lax.map(one_block, jnp.arange(seq_len // block_size, dtype=jnp.int32))
    return (contexts.reshape(queries.shape), log_sums)


def attend_backward(row_items):
    queries, key_rows, value_rows, seg_row, valid_row, log_sums, d_context = row_items
    seq_len = queries.shape[0]
    block_size = min(512, seq_len)
    score_scale = 1.0 / math.sqrt(HEAD_DIM)
    zero_keys = jnp.zeros(key_rows.shape, jnp.float32)

    def one_block(totals, block_index):
        key_total, value_total = totals
        block_start = block_index * block_size
        query_block = lax.dynamic_slice_in_dim(queries, block_start, block_size, 0)
        grad_block = lax.dynamic_slice_in_dim(d_context, block_start, block_size, 0)
        allowed = allowed_block(seg_row, valid_row, block_start, block_size)
        scores = block_scores(query_block, key_rows, allowed, score_scale)
        weights = jnp.where(allowed[None], jnp.exp(scores - log_sums[block_index][:, :, None]), 0.0)
        low_weights = weights.astype(jnp.bfloat16)
        d_weights = jnp.einsum(
            "qhd,khd->hqk", grad_block, value_rows, preferred_element_type=jnp.float32
        )
        row_delta = jnp.sum(weights * d_weights, axis=2, keepdims=True)
        d_scores = (weights * (d_weights - row_delta)).astype(jnp.bfloat16)
        d_query = (
            jnp.einsum("hqk,khd->qhd", d_scores, key_rows, preferred_element_type=jnp.float32)
            * score_scale
        )
        key_total = (
            key_total
            + jnp.einsum("hqk,qhd->khd", d_scores, query_block, preferred_element_type=jnp.float32)
            * score_scale
        )
        value_total = value_total + jnp.einsum(
            "hqk,qhd->khd", low_weights, grad_block, preferred_element_type=jnp.float32
        )
        return ((key_total, value_total), d_query.astype(jnp.bfloat16))

    (key_total, value_total), d_queries = lax.scan(
        one_block, (zero_keys, zero_keys), jnp.arange(seq_len // block_size, dtype=jnp.int32)
    )
    return (
        d_queries.reshape(queries.shape),
        key_total.astype(jnp.bfloat16),
        value_total.astype(jnp.bfloat16),
    )


def local(
    inputs,
    segments,
    valid,
    w_query,
    b_query,
    w_key,
    w_value,
    b_value,
    w_out,
    b_out,
    gain_one,
    shift_one,
    w_up,
    b_up,
    w_down,
    b_down,
    gain_two,
    shift_two,
    lex_weight,
    lex_bias,
    cotangent,
):
    row_count, seq_len, full_width = inputs.shape
    token_count = row_count * seq_len
    slice_width = full_width // lax.axis_size("tensor")
    offset = lax.axis_index("tensor") * slice_width
    local_width = w_query.shape[1]
    heads_here = local_width // HEAD_DIM
    flat = inputs.reshape(token_count, full_width)
    own_input = lax.dynamic_slice_in_dim(flat, offset, slice_width, 1).astype(jnp.float32)
    queries = (jnp.dot(flat, w_query, preferred_element_type=jnp.float32) + b_query).astype(
        jnp.bfloat16
    )
    key_rows = jnp.dot(flat, w_key, preferred_element_type=jnp.float32).astype(jnp.bfloat16)
    value_rows = (jnp.dot(flat, w_value, preferred_element_type=jnp.float32) + b_value).astype(
        jnp.bfloat16
    )
    head_shape = (row_count, seq_len, heads_here, HEAD_DIM)
    query_heads = queries.reshape(head_shape)
    key_heads = key_rows.reshape(head_shape)
    value_heads = value_rows.reshape(head_shape)
    contexts, log_sums = lax.map(
        attend_forward, (query_heads, key_heads, value_heads, segments, valid)
    )
    context = contexts.reshape(token_count, local_width)
    out_cols = lax.all_to_all(w_out, "tensor", split_axis=1, concat_axis=0, tiled=True)
    attended = jnp.dot(
        lax.all_gather(context, "tensor", axis=1, tiled=True),
        out_cols,
        preferred_element_type=jnp.float32,
    )
    first_res = own_input + attended + b_out
    sum_one, square_one = (
        lax.psum(jnp.sum(first_res, axis=1).astype(jnp.bfloat16), "tensor").astype(jnp.float32),
        lax.psum(jnp.sum(first_res * first_res, axis=1).astype(jnp.bfloat16), "tensor").astype(
            jnp.float32
        ),
    )
    mean_one, scale_one = norm_from_sums(sum_one, square_one, full_width)
    normed_one = (first_res - mean_one[:, None]) * scale_one[:, None]
    first_out = normed_one * gain_one + shift_one
    first_low = first_out.astype(jnp.bfloat16)
    first_all = lax.all_gather(first_low, "tensor", axis=1, tiled=True)
    pre_up = jnp.dot(first_all, w_up, preferred_element_type=jnp.float32) + b_up
    hidden = gelu_exact(pre_up).astype(jnp.bfloat16)
    ffn_term = jnp.dot(hidden, w_down, preferred_element_type=jnp.float32)
    ffn_out = lax.psum_scatter(
        ffn_term.astype(jnp.bfloat16), "tensor", scatter_dimension=1, tiled=True
    ).astype(jnp.float32)
    second_res = first_out + ffn_out + b_down
    lex_gain = gain_two * lex_weight
    sum_two, square_two, lex_cross, lex_const = (
        lax.psum(jnp.sum(second_res, axis=1).astype(jnp.bfloat16), "tensor").astype(jnp.float32),
        lax.psum(jnp.sum(second_res * second_res, axis=1).astype(jnp.bfloat16), "tensor").astype(
            jnp.float32
        ),
        lax.psum(jnp.sum(second_res * lex_gain, axis=1).astype(jnp.bfloat16), "tensor").astype(
            jnp.float32
        ),
        lax.psum(
            jnp.stack(
                [
                    jnp.sum(lex_gain.astype(jnp.float32)),
                    jnp.sum((shift_two * lex_weight).astype(jnp.float32)),
                ]
            ).astype(jnp.bfloat16),
            "tensor",
        ).astype(jnp.float32),
    )
    mean_two, scale_two = norm_from_sums(sum_two, square_two, full_width)
    normed_two = (second_res - mean_two[:, None]) * scale_two[:, None]
    final_out = normed_two * gain_two + shift_two
    output = final_out.astype(jnp.bfloat16).reshape(row_count, seq_len, slice_width)
    lex_pre = (
        scale_two * (lex_cross - mean_two * lex_const[0])
        + lex_const[1]
        + lex_bias[0].astype(jnp.float32)
    )
    lex_values = jnp.maximum(lex_pre, 0.0)
    lex_above = jnp.where(lex_pre > 0.0, 1.0, 0.0).astype(jnp.float32)
    valid_float = valid.reshape(token_count).astype(jnp.float32)
    lex_totals = jnp.stack(
        [jnp.sum(valid_float), jnp.sum(lex_values * valid_float), jnp.sum(lex_above * valid_float)]
    )
    d_final = cotangent.reshape(token_count, slice_width).astype(jnp.float32)
    grad_gain_two = jnp.sum(d_final * normed_two, axis=0)
    grad_shift_two = jnp.sum(d_final, axis=0)
    d_scaled_two = d_final * gain_two
    back_sum_two, back_cross_two = (
        lax.psum(jnp.sum(d_scaled_two, axis=1).astype(jnp.bfloat16), "tensor").astype(jnp.float32),
        lax.psum(jnp.sum(d_scaled_two * normed_two, axis=1).astype(jnp.bfloat16), "tensor").astype(
            jnp.float32
        ),
    )
    d_second = scale_two[:, None] * (
        d_scaled_two
        - back_sum_two[:, None] / full_width
        - normed_two * back_cross_two[:, None] / full_width
    )
    grad_b_down = jnp.sum(d_second, axis=0)
    d_ffn_low = d_second.astype(jnp.bfloat16)
    shard_piece = lax.all_gather(d_ffn_low, "tensor", axis=1, tiled=True)
    column_block = w_down
    hidden_total = inner_last(shard_piece, column_block)
    weight_total = inner_first(hidden, shard_piece)
    grad_w_down = weight_total
    _, gelu_back = jax.vjp(gelu_exact, pre_up)
    d_pre_up = gelu_back(hidden_total)[0].astype(jnp.bfloat16)
    grad_b_up = jnp.sum(d_pre_up, axis=0, dtype=jnp.float32)
    grad_w_up = inner_first(lax.all_gather(first_low, "tensor", axis=1, tiled=True), d_pre_up)
    d_first_term = inner_last(d_pre_up, w_up)
    d_first = (
        lax.psum_scatter(
            d_first_term.astype(jnp.bfloat16), "tensor", scatter_dimension=1, tiled=True
        ).astype(jnp.float32)
        + d_second
    )
    grad_gain_one = jnp.sum(d_first * normed_one, axis=0)
    grad_shift_one = jnp.sum(d_first, axis=0)
    d_scaled_one = d_first * gain_one
    back_sum_one, back_cross_one = (
        lax.psum(jnp.sum(d_scaled_one, axis=1).astype(jnp.bfloat16), "tensor").astype(jnp.float32),
        lax.psum(jnp.sum(d_scaled_one * normed_one, axis=1).astype(jnp.bfloat16), "tensor").astype(
            jnp.float32
        ),
    )
    d_first_res = scale_one[:, None] * (
        d_scaled_one
        - back_sum_one[:, None] / full_width
        - normed_one * back_cross_one[:, None] / full_width
    )
    grad_b_out = jnp.sum(d_first_res, axis=0)
    d_attn_low = d_first_res.astype(jnp.bfloat16)
    shard_piece = lax.all_gather(d_attn_low, "tensor", axis=1, tiled=True)
    column_block = w_out
    context_total = inner_last(shard_piece, column_block)
    weight_total = inner_first(context, shard_piece)
    d_context_heads = context_total.astype(jnp.bfloat16).reshape(head_shape)
    d_query_heads, d_key_heads, d_value_heads = lax.map(
        attend_backward,
        (query_heads, key_heads, value_heads, segments, valid, log_sums, d_context_heads),
    )
    d_queries = d_query_heads.reshape(token_count, local_width)
    d_keys = d_key_heads.reshape(token_count, local_width)
    d_values = d_value_heads.reshape(token_count, local_width)
    grad_w_query = inner_first(flat, d_queries)
    grad_w_key = inner_first(flat, d_keys)
    grad_w_value = inner_first(flat, d_values)
    grad_b_query = jnp.sum(d_queries, axis=0, dtype=jnp.float32)
    grad_b_value = jnp.sum(d_values, axis=0, dtype=jnp.float32)
    d_input_term = (
        inner_last(d_queries, w_query) + inner_last(d_keys, w_key) + inner_last(d_values, w_value)
    )
    d_input = (
        lax.psum_scatter(
            d_input_term.astype(jnp.bfloat16), "tensor", scatter_dimension=1, tiled=True
        ).astype(jnp.float32)
        + d_first_res
    )
    grad_inputs = d_input.astype(jnp.bfloat16).reshape(row_count, seq_len, slice_width)
    summed = (
        lax.psum(grad_w_query.astype(jnp.bfloat16), "batch").astype(jnp.float32),
        lax.psum(grad_b_query.astype(jnp.bfloat16), "batch").astype(jnp.float32),
        lax.psum(grad_w_key.astype(jnp.bfloat16), "batch").astype(jnp.float32),
        lax.psum(grad_w_value.astype(jnp.bfloat16), "batch").astype(jnp.float32),
        lax.psum(grad_b_value.astype(jnp.bfloat16), "batch").astype(jnp.float32),
        lax.psum(weight_total.astype(jnp.bfloat16), "batch").astype(jnp.float32),
        lax.psum(grad_b_out.astype(jnp.bfloat16), "batch").astype(jnp.float32),
        lax.psum(grad_gain_one.astype(jnp.bfloat16), "batch").astype(jnp.float32),
        lax.psum(grad_shift_one.astype(jnp.bfloat16), "batch").astype(jnp.float32),
        lax.psum(grad_w_up.astype(jnp.bfloat16), "batch").astype(jnp.float32),
        lax.psum(grad_b_up.astype(jnp.bfloat16), "batch").astype(jnp.float32),
        lax.psum(grad_w_down.astype(jnp.bfloat16), "batch").astype(jnp.float32),
        lax.psum(grad_b_down.astype(jnp.bfloat16), "batch").astype(jnp.float32),
        lax.psum(grad_gain_two.astype(jnp.bfloat16), "batch").astype(jnp.float32),
        lax.psum(grad_shift_two.astype(jnp.bfloat16), "batch").astype(jnp.float32),
        lax.psum(lex_totals.astype(jnp.bfloat16), "batch").astype(jnp.float32),
    )
    totals_all = summed[15]
    lex_stats = jnp.stack([totals_all[1] / totals_all[0], totals_all[2] / totals_all[0]])
    return (
        output,
        grad_inputs,
        summed[0],
        summed[1],
        summed[2],
        summed[3],
        summed[4],
        summed[5],
        summed[6],
        summed[7],
        summed[8],
        summed[9],
        summed[10],
        summed[11],
        summed[12],
        summed[13],
        summed[14],
        lex_stats,
    )


def solution(mesh):
    in_specs = (
        P("batch", None, None),
        P("batch", None),
        P("batch", None),
        P(None, "tensor"),
        P("tensor"),
        P(None, "tensor"),
        P(None, "tensor"),
        P("tensor"),
        P("tensor", None),
        P("tensor"),
        P("tensor"),
        P("tensor"),
        P(None, "tensor"),
        P("tensor"),
        P("tensor", None),
        P("tensor"),
        P("tensor"),
        P("tensor"),
        P("tensor"),
        P(),
        P("batch", None, "tensor"),
    )
    out_specs = (
        P("batch", None, "tensor"),
        P("batch", None, "tensor"),
        P(None, "tensor"),
        P("tensor"),
        P(None, "tensor"),
        P(None, "tensor"),
        P("tensor"),
        P("tensor", None),
        P("tensor"),
        P("tensor"),
        P("tensor"),
        P(None, "tensor"),
        P("tensor"),
        P("tensor", None),
        P("tensor"),
        P("tensor"),
        P("tensor"),
        P(),
    )
    return jax.shard_map(local, mesh=mesh, in_specs=in_specs, out_specs=out_specs, check_vma=False)
```

profile of v0, /device:TPU:0, one launch (start us, length us, event | category | flops | bytes accessed | tf_op | source)
XLA Modules:
  0.0 2700.3 jit_solution(17977070279879198064)
XLA Ops:
  25.4 421.0 %while.47 = (s32[]{:T(128)}, bf16[8,512,4,64]{1,3,2,0:T(8,128)(2,1)}, f32[8,4,512]{2,1,0:T(4,128)}, s32[8]{0:T(128)S(1)}, s32[4096]{0:T(1024)S(1)}, /*index=5*/s...) while((s32[]{:T(128)}, ...), condition=%wide.region_3.4_spmd, body=%wide.region_0.3_spmd.sunk | while | flops 2256669184 | bytes 122276080 | solution.py:73
  60.7 16.9 fusion.169
  165.8 16.9 fusion.169
  483.6 125.4 %all-gather.5.cloned.1.call-done = bf16[4096,1024]{0,1:T(8,128)(2,1)} async-done(((bf16[4096,256]{0,1:T(8,128)(2,1)}), bf16[4096,1024]{0,1:T(8,128)(2,1)}) %all-gather.5.cloned.1.call-update) | async-done | bytes 8388624 | tf_op jit(solution)/shard_map/all_gather | solution.py:170
  639.5 147.9 %all-gather.7.cloned.1.call-done = bf16[4096,1024]{0,1:T(8,128)(2,1)} async-done(((bf16[4096,256]{0,1:T(8,128)(2,1)}), bf16[4096,1024]{0,1:T(8,128)(2,1)}) %all-gather.7.cloned.1.call-update) | async-done | bytes 8388624 | tf_op jit(solution)/shard_map/all_gather | solution.py:185
  787.4 17.0 multiply_convert_fusion.1
  824.4 137.6 %reduce-scatter.4.cloned.1.call-done = bf16[4096,256]{0,1:T(8,128)(2,1)} async-done(((bf16[4096,1024]{0,1:T(8,128)(2,1)}), bf16[4096,256]{0,1:T(8,128)(2,1)}) %reduce-scatter.4.cloned.1.call-update) | async-done | bytes 2097168 | tf_op jit(solution)/shard_map/reduce_scatter | solution.py:189
  968.5 18.1 all-reduce.4
  1012.9 148.5 %all-gather.9.cloned.1.call-done = bf16[4096,1024]{0,1:T(8,128)(2,1)} async-done(((bf16[4096,256]{0,1:T(8,128)(2,1)}), bf16[4096,1024]{0,1:T(8,128)(2,1)}) %all-gather.9.cloned.1.call-update) | async-done | bytes 8388624 | tf_op jit(solution)/shard_map/all_gather | solution.py:244
  1161.4 20.6 fusion.98
  1198.2 140.9 %reduce-scatter.6.cloned.1.call-done = bf16[4096,256]{0,1:T(8,128)(2,1)} async-done(((bf16[4096,1024]{0,1:T(8,128)(2,1)}), bf16[4096,256]{0,1:T(8,128)(2,1)}) %reduce-scatter.6.cloned.1.call-update) | async-done | bytes 2097168 | tf_op jit(solution)/shard_map/reduce_scatter | solution.py:255
  1345.9 18.8 all-reduce.2
  1406.3 118.5 %all-gather.11.cloned.1.call-done = bf16[4096,1024]{0,1:T(8,128)(2,1)} async-done(((bf16[4096,256]{0,1:T(8,128)(2,1)}), bf16[4096,1024]{0,1:T(8,128)(2,1)}) %all-gather.11.cloned.1.call-update) | async-done | bytes 8388624 | tf_op jit(solution)/shard_map/all_gather | solution.py:276
  1533.5 878.7 %while.48 = (s32[]{:T(128)}, f32[4096,4,64]{0,2,1:T(8,128)}, f32[4096,4,64]{0,2,1:T(8,128)}, bf16[8,512,4,64]{1,3,2,0:T(8,128)(2,1)}, s32[8]{0:T(128)S(1)}, /*in...) while((s32[]{:T(128)}, f32[4096,4,64]{0,2,1:T(8,128)}, ...), condition=%wide.region_24.25_spmd.clone, body=%wide.region_22.24_spmd.clone.sunk | while | flops 5466491392 | bytes 355821888 | solution.py:112
  1554.6 25.9 multiply_reduce_fusion.12
  1580.5 27.7 %multiply_convert_fusion.4 = bf16[4,512,4096]{2,1,0:T(8,128)(2,1)} fusion(f32[4,512,4096]{2,1,0:T(8,128)} %get-tuple-element.535, f32[4,512,4096]{2,1,0:T(8,128)} %fusion.179, f32[4,512]{1,0:T(4,128)S(1)} %get-tuple-element.536), kind=kLoop, calls=%fused_computation.19.clone.1 | loop fusion | flops 25165824 | bytes 83894272 | tf_op jit(solution)/shard_map/while/body/eval_jaxpr/while/body/eval_jaxpr/convert_element_type | solution.py:97
  1662.2 25.9 multiply_reduce_fusion.12
  1688.1 27.7 %multiply_convert_fusion.4 = bf16[4,512,4096]{2,1,0:T(8,128)(2,1)} fusion(f32[4,512,4096]{2,1,0:T(8,128)} %get-tuple-element.535, f32[4,512,4096]{2,1,0:T(8,128)} %fusion.179, f32[4,512]{1,0:T(4,128)S(1)} %get-tuple-element.536), kind=kLoop, calls=%fused_computation.19.clone.1 | loop fusion | flops 25165824 | bytes 83894272 | tf_op jit(solution)/shard_map/while/body/eval_jaxpr/while/body/eval_jaxpr/convert_element_type | solution.py:97
  1772.3 25.9 multiply_reduce_fusion.12
  1798.2 27.7 %multiply_convert_fusion.4 = bf16[4,512,4096]{2,1,0:T(8,128)(2,1)} fusion(f32[4,512,4096]{2,1,0:T(8,128)} %get-tuple-element.535, f32[4,512,4096]{2,1,0:T(8,128)} %fusion.179, f32[4,512]{1,0:T(4,128)S(1)} %get-tuple-element.536), kind=kLoop, calls=%fused_computation.19.clone.1 | loop fusion | flops 25165824 | bytes 83894272 | tf_op jit(solution)/shard_map/while/body/eval_jaxpr/while/body/eval_jaxpr/convert_element_type | solution.py:97
  1882.4 25.9 multiply_reduce_fusion.12
  1908.3 27.7 %multiply_convert_fusion.4 = bf16[4,512,4096]{2,1,0:T(8,128)(2,1)} fusion(f32[4,512,4096]{2,1,0:T(8,128)} %get-tuple-element.535, f32[4,512,4096]{2,1,0:T(8,128)} %fusion.179, f32[4,512]{1,0:T(4,128)S(1)} %get-tuple-element.536), kind=kLoop, calls=%fused_computation.19.clone.1 | loop fusion | flops 25165824 | bytes 83894272 | tf_op jit(solution)/shard_map/while/body/eval_jaxpr/while/body/eval_jaxpr/convert_element_type | solution.py:97
  1992.5 25.9 multiply_reduce_fusion.12
  2018.4 27.7 %multiply_convert_fusion.4 = bf16[4,512,4096]{2,1,0:T(8,128)(2,1)} fusion(f32[4,512,4096]{2,1,0:T(8,128)} %get-tuple-element.535, f32[4,512,4096]{2,1,0:T(8,128)} %fusion.179, f32[4,512]{1,0:T(4,128)S(1)} %get-tuple-element.536), kind=kLoop, calls=%fused_computation.19.clone.1 | loop fusion | flops 25165824 | bytes 83894272 | tf_op jit(solution)/shard_map/while/body/eval_jaxpr/while/body/eval_jaxpr/convert_element_type | solution.py:97
  2102.6 25.9 multiply_reduce_fusion.12
  2128.5 27.7 %multiply_convert_fusion.4 = bf16[4,512,4096]{2,1,0:T(8,128)(2,1)} fusion(f32[4,512,4096]{2,1,0:T(8,128)} %get-tuple-element.535, f32[4,512,4096]{2,1,0:T(8,128)} %fusion.179, f32[4,512]{1,0:T(4,128)S(1)} %get-tuple-element.536), kind=kLoop, calls=%fused_computation.19.clone.1 | loop fusion | flops 25165824 | bytes 83894272 | tf_op jit(solution)/shard_map/while/body/eval_jaxpr/while/body/eval_jaxpr/convert_element_type | solution.py:97
  2212.7 25.9 multiply_reduce_fusion.12
  2238.6 27.7 %multiply_convert_fusion.4 = bf16[4,512,4096]{2,1,0:T(8,128)(2,1)} fusion(f32[4,512,4096]{2,1,0:T(8,128)} %get-tuple-element.535, f32[4,512,4096]{2,1,0:T(8,128)} %fusion.179, f32[4,512]{1,0:T(4,128)S(1)} %get-tuple-element.536), kind=kLoop, calls=%fused_computation.19.clone.1 | loop fusion | flops 25165824 | bytes 83894272 | tf_op jit(solution)/shard_map/while/body/eval_jaxpr/while/body/eval_jaxpr/convert_element_type | solution.py:97
  2322.8 25.9 multiply_reduce_fusion.12
  2348.7 27.7 %multiply_convert_fusion.4 = bf16[4,512,4096]{2,1,0:T(8,128)(2,1)} fusion(f32[4,512,4096]{2,1,0:T(8,128)} %get-tuple-element.535, f32[4,512,4096]{2,1,0:T(8,128)} %fusion.179, f32[4,512]{1,0:T(4,128)S(1)} %get-tuple-element.536), kind=kLoop, calls=%fused_computation.19.clone.1 | loop fusion | flops 25165824 | bytes 83894272 | tf_op jit(solution)/shard_map/while/body/eval_jaxpr/while/body/eval_jaxpr/convert_element_type | solution.py:97
  2502.2 34.7 %all-reduce.8.cloned.1.call-done = (bf16[1024,256]{0,1:T(8,128)(2,1)}, bf16[1024,256]{0,1:T(8,128)(2,1)}, bf16[1024,256]{0,1:T(8,128)(2,1)}, bf16[256,1024]{1,0:...) async-done(((bf16[1024,256]{0,1:T(8,128)(2,1)}, bf16[1024,256]{0,1:T(8,128)(2,1)}, bf16[1024,256]{0,1:T(8,128)(2,1)}, bf16[256,1024]{1,0:T(8,128)(2,1)}, ...) | async-done | bytes 6291472 | tf_op jit(solution)/shard_map/psum | solution.py:304
  2552.0 132.1 %reduce-scatter.8.cloned.1.call-done = bf16[4096,256]{0,1:T(8,128)(2,1)} async-done(((bf16[4096,1024]{0,1:T(8,128)(2,1)}), bf16[4096,256]{0,1:T(8,128)(2,1)}) %reduce-scatter.8.cloned.1.call-update) | async-done | bytes 2097168 | tf_op jit(solution)/shard_map/reduce_scatter | solution.py:297
  (390 shorter events, 1130.9 us)
Async XLA Ops:
  7.2 780.2 %copy-start = (bf16[1024,1024]{1,0:T(8,128)(2,1)S(1)}, bf16[1024,1024]{1,0:T(8,128)(2,1)}, u32[]{:S(2)}) copy-start(bf16[1024,1024]{1,0:T(8,128)(2,1)} %param.37) | copy-start | bytes 6291460
  7.2 601.7 %all-gather.5.cloned.1.call-start = ((), (), s32[]{:S(2)}) async-start(), calls=%async_computation.4 | async-start | bytes 10485760 | tf_op jit(solution)/shard_map/all_gather | solution.py:170
  29.7 15.9 copy-start.4
  82.3 15.9 copy-start.4
  134.8 15.9 copy-start.4
  187.4 15.9 copy-start.4
  239.9 15.9 copy-start.4
  292.5 15.9 copy-start.4
  345.0 15.9 copy-start.4
  397.6 15.9 copy-start.4
  452.5 30.1 %all-to-all-start = ((bf16[256,4,256]{0,2,1:T(8,128)(2,1)}), bf16[256,4,256]{0,2,1:T(8,128)(2,1)S(1)}, u32[]{:S(2)}, u32[]{:S(2)}) async-start(bf16[256,4,256]{0,2,1:T(8,128)(2,1)} %bitcast.11), calls=%async_computation | async-start | bytes 1048576 | tf_op jit(solution)/shard_map/all_to_all | solution.py:168
  458.8 328.6 %all-gather.7.cloned.1.call-start = ((), (), s32[]{:S(2)}) async-start(), calls=%async_computation.5 | async-start | bytes 10485760 | tf_op jit(solution)/shard_map/all_gather | solution.py:185
  639.4 322.5 %reduce-scatter.4.cloned.1.call-start = ((), (), s32[]{:S(2)}) async-start(), calls=%async_computation.6 | async-start | bytes 10485760 | tf_op jit(solution)/shard_map/reduce_scatter | solution.py:189
  787.4 17.0 copy-start.39
  819.1 342.3 %all-gather.9.cloned.1.call-start = ((), (), s32[]{:S(2)}) async-start(), calls=%async_computation.7 | async-start | bytes 10485760 | tf_op jit(solution)/shard_map/all_gather | solution.py:244
  1012.8 326.2 %reduce-scatter.6.cloned.1.call-start = ((), (), s32[]{:S(2)}) async-start(), calls=%async_computation.8 | async-start | bytes 10485760 | tf_op jit(solution)/shard_map/reduce_scatter | solution.py:255
  1196.1 328.7 %all-gather.11.cloned.1.call-start = ((), (), s32[]{:S(2)}) async-start(), calls=%async_computation.9 | async-start | bytes 10485760 | tf_op jit(solution)/shard_map/all_gather | solution.py:276
  1339.1 28.2 %copy-start.11 = (bf16[4096,256]{0,1:T(8,128)(2,1)S(1)}, bf16[4096,256]{0,1:T(8,128)(2,1)}, u32[]{:S(2)}) copy-start(bf16[4096,256]{0,1:T(8,128)(2,1)} %reduce-scatter.6.cloned.1.call-done) | copy-start | bytes 6291460
  1376.6 1160.3 %all-reduce.8.cloned.1.call-start = ((), (), s32[]{:S(2)}) async-start(), calls=%async_computation.11 | async-start | bytes 12582912 | tf_op jit(solution)/shard_map/psum | solution.py:304
  1391.5 133.3 %copy-start.28 = (bf16[256,1024]{1,0:T(8,128)(2,1)S(1)}, bf16[256,1024]{1,0:T(8,128)(2,1)}, u32[]{:S(2)}) copy-start(bf16[256,1024]{1,0:T(8,128)(2,1)} %param.33) | copy-start | bytes 1572868
  1406.3 127.1 %copy-start.5 = (bf16[4096,4,64]{0,2,1:T(8,128)(2,1)S(1)}, bf16[4096,4,64]{0,2,1:T(8,128)(2,1)}, u32[]{:S(2)}) copy-start(bf16[4096,4,64]{0,2,1:T(8,128)(2,1)} %get-tuple-element.646) | copy-start | bytes 6291460
  1406.3 127.1 %copy-start.17 = (s32[1,4096]{1,0:T(1,128)S(1)}, s32[1,4096]{1,0:T(1,128)}, u32[]{:S(2)}) copy-start(s32[1,4096]{1,0:T(1,128)} %param.26) | copy-start | bytes 49156
  1540.4 14.2 copy-start.6
  1623.9 11.2 copy-start.2
  1647.9 14.2 copy-start.6
  1758.1 14.2 copy-start.6
  1868.2 14.2 copy-start.6
  1978.3 14.2 copy-start.6
  2088.4 14.2 copy-start.6
  2198.5 14.2 copy-start.6
  2308.6 14.2 copy-start.6
  2434.3 249.8 %reduce-scatter.8.cloned.1.call-start = ((), (), s32[]{:S(2)}) async-start(), calls=%async_computation.10 | async-start | bytes 10485760 | tf_op jit(solution)/shard_map/reduce_scatter | solution.py:297
  (45 other events, 305.9 us)
Sparse Core Ops, SparseCore 0:
  451.6 157.2 all-gather.4
  639.6 147.7 all-gather.6
  819.1 142.7 reduce-scatter.3
  1013.0 148.3 all-gather.8
  1196.2 142.7 reduce-scatter.5
  1376.8 148.0 all-gather.10
  2434.4 102.5 all-reduce.7
  2539.3 144.7 reduce-scatter.7
where the time goes:
time: 2710 us; the launch traced here: 2700 us
  matrix products  1030 us (38%)
  waiting for transfers between devices  1000 us (37%)
  other arithmetic  458 us (17%)
  blocking collectives  84 us (3%)
  local copies, waits for them, and re-layouts  75.9 us (3%)
  loops' own time  27.4 us (1%)
    dot_general x16, matrix products, block_scores(): jnp.einsum('qhd,khd->hqk', query_block, key_rows, preferred_element_type=...  335 us
    convert_element_type x8, other arithmetic, one_block(): d_scores = (weights * (d_weights - row_delta)).astype(jnp.bfloat16)  222 us
    all_gather x1, waiting for transfers between devices, local(): shard_piece = lax.all_gather(d_ffn_low, 'tensor', axis=1, tiled=True)  148 us
    all_gather x1, waiting for transfers between devices, local(): first_all = lax.all_gather(first_low, 'tensor', axis=1, tiled=True)  148 us
    reduce_scatter x1, waiting for transfers between devices, local(): lax.psum_scatter(d_first_term.astype(jnp.bfloat16), 'tensor', scatter_dim...  141 us
    reduce_scatter x1, waiting for transfers between devices, local(): lax.psum_scatter(ffn_term.astype(jnp.bfloat16), 'tensor', scatter_dimensi...  138 us
    dot_general x8, matrix products, one_block(): jnp.einsum('hqk,khd->qhd', weights, value_rows, preferred_element_type=jn...  135 us
    dot_general x8, matrix products, one_block(): jnp.einsum('hqk,qhd->khd', low_weights, grad_block, preferred_element_typ...  134 us
  transfers between devices with their start and end apart: 9, of which 9 were waited for; matrix products, arithmetic and copies ran while one was open for 4% of the time, Pallas kernels for 0%

commit v1 on v0

v1 whole, which is shorter than its diff:
```python
import math, functools
import jax
import jax.numpy as jnp
from jax import lax
from jax.experimental import pallas as pl
from jax.experimental.pallas import tpu as pltpu

HEAD_DIM = 64
MASKED = -1e30
NT = (((1,), (1,)), ((), ()))
NN = (((1,), (0,)), ((), ()))


def dot_f32(left, right, dims):
    return lax.dot_general(left, right, dims, preferred_element_type=jnp.float32)


def head_lanes(shape, slot):
    lane = lax.broadcasted_iota(jnp.int32, shape, 1)
    return (lane >= slot * HEAD_DIM) & (lane < (slot + 1) * HEAD_DIM)


def pick_head(block, head, pair_width):
    group, slot = divmod(head * HEAD_DIM, pair_width)
    pair = block[:, group * pair_width : (group + 1) * pair_width]
    if pair_width == HEAD_DIM:
        return pair
    return jnp.where(head_lanes(pair.shape, slot // HEAD_DIM), pair, jnp.zeros_like(pair))


def allowed_tile(key_start, query_start, low_row, high_row, size):
    key_pos = key_start + lax.broadcasted_iota(jnp.int32, (size, 1), 0)
    query_pos = query_start + lax.broadcasted_iota(jnp.int32, (1, size), 1)
    return ((key_pos >= low_row) & (key_pos < high_row)) | (key_pos == query_pos)


def forward_body(
    first_block, size, heads, pair_width,
    bounds_ref, q_ref, k_ref, vt_ref, low_ref, high_ref,
    ctx_ref, lse_ref,
    qh_ref, acc_ref, max_ref, sum_ref,
):
    block = first_block + pl.program_id(0)
    for head in range(heads):
        qh_ref[head] = pick_head(q_ref[...], head, pair_width) * jnp.bfloat16(0.125)
    acc_ref[...] = jnp.zeros_like(acc_ref)
    max_ref[...] = jnp.full_like(max_ref, MASKED)
    sum_ref[...] = jnp.zeros_like(sum_ref)
    low_first, low_last = bounds_ref[0, block], bounds_ref[1, block]
    high_first, high_last = bounds_ref[2, block], bounds_ref[3, block]
    lower = low_first // size
    count = jnp.maximum((high_last + size - 1) // size - lower, 0)
    extra = jnp.where(block < lower + count, 0, 1)

    def visit(key_block, masked):
        key_start = pl.multiple_of(key_block * size, size)
        keys = pl.ds(key_start, size)
        if masked:
            allowed = allowed_tile(
                key_start, block * size, low_ref[...], high_ref[...], size
            )
        for head in range(heads):
            base = head * HEAD_DIM // pair_width * pair_width
            scores = dot_f32(k_ref[keys, base : base + pair_width], qh_ref[head], NT)
            if masked:
                scores = jnp.where(allowed, scores, MASKED)
            old_max = max_ref[head]
            new_max = jnp.maximum(old_max, jnp.max(scores, axis=0, keepdims=True))
            expo = jnp.exp(scores - new_max)
            scale = jnp.exp(old_max - new_max)
            max_ref[head] = new_max
            sum_ref[head] = sum_ref[head] * scale + jnp.sum(expo, axis=0, keepdims=True)
            rows = slice(head * HEAD_DIM, (head + 1) * HEAD_DIM)
            acc_ref[rows, :] = acc_ref[rows, :] * scale + dot_f32(
                vt_ref[rows, keys], expo.astype(jnp.bfloat16), NN
            )

    def step(index, carry):
        key_block = jnp.where(index < count, lower + index, block)
        key_start = key_block * size
        full = (key_start >= low_last) & (key_start + size <= high_first)
        pl.when(full)(lambda: visit(key_block, False))
        pl.when(jnp.logical_not(full))(lambda: visit(key_block, True))
        return carry

    lax.fori_loop(0, count + extra, step, 0)
    for head in range(heads):
        rows = slice(head * HEAD_DIM, (head + 1) * HEAD_DIM)
        acc_ref[rows, :] = acc_ref[rows, :] / sum_ref[head]
        lse_ref[head : head + 1, :] = max_ref[head] + jnp.log(sum_ref[head])
    ctx_ref[...] = acc_ref[...].T.astype(jnp.bfloat16)


def block_size_of(tokens):
    return min(256, tokens)


def attend_forward(q, k, vt, low, high, bounds, first=0, last=None):
    tokens, width = q.shape
    size = block_size_of(tokens)
    heads = width // HEAD_DIM
    pair_width = min(128, width)
    last = tokens // size if last is None else last
    grid = last - first
    row_spec = pl.BlockSpec((1, size), lambda i, b: (0, i + first))
    return pl.pallas_call(
        functools.partial(forward_body, first, size, heads, pair_width),
        name="attend_forward",
        out_shape=(
            jax.ShapeDtypeStruct((grid * size, width), jnp.bfloat16),
            jax.ShapeDtypeStruct((heads, grid * size), jnp.float32),
        ),
        grid_spec=pltpu.PrefetchScalarGridSpec(
            num_scalar_prefetch=1,
            grid=(grid,),
            in_specs=[
                pl.BlockSpec((size, width), lambda i, b: (i + first, 0)),
                pl.BlockSpec((tokens, width), lambda i, b: (0, 0), pipeline_mode=pl.Buffered(1)),
                pl.BlockSpec((width, tokens), lambda i, b: (0, 0), pipeline_mode=pl.Buffered(1)),
                row_spec,
                row_spec,
            ],
            out_specs=[
                pl.BlockSpec((size, width), lambda i, b: (i, 0)),
                pl.BlockSpec((heads, size), lambda i, b: (0, i)),
            ],
            scratch_shapes=[
                pltpu.VMEM((heads, size, pair_width), jnp.bfloat16),
                pltpu.VMEM((width, size), jnp.float32),
                pltpu.VMEM((heads, 1, size), jnp.float32),
                pltpu.VMEM((heads, 1, size), jnp.float32),
            ],
        ),
        compiler_params=pltpu.CompilerParams(vmem_limit_bytes=40 << 20),
    )(bounds, q, k, vt, low, high)


def backward_body(
    size, heads, pair_width,
    bounds_ref, q_ref, k_ref, v_ref, kt_ref, do_ref, ctx_ref, lse_ref, low_ref, high_ref,
    dq_ref, dk_ref, dv_ref,
    qh_ref, doh_ref, delta_ref, dqt_ref, dk_acc, dv_acc,
):
    block = pl.program_id(0)
    blocks = pl.num_programs(0)
    groups = heads * HEAD_DIM // pair_width

    @pl.when(block == 0)
    def _():
        dqt_ref[...] = jnp.zeros_like(dqt_ref)

        def prepare(index, carry):
            rows = pl.ds(pl.multiple_of(index * size, size), size)
            for head in range(heads):
                qh_ref[head, rows, :] = pick_head(q_ref[rows, :], head, pair_width) * jnp.bfloat16(0.125)
                doh_ref[head, rows, :] = pick_head(do_ref[rows, :], head, pair_width)
            both = (do_ref[rows, :].astype(jnp.float32) * ctx_ref[rows, :].astype(jnp.float32)).T
            for head in range(heads):
                part = both[head * HEAD_DIM : (head + 1) * HEAD_DIM, :]
                delta_ref[head, :, rows] = jnp.sum(part, axis=0, keepdims=True)
            return carry

        lax.fori_loop(0, blocks, prepare, 0)

    dk_acc[...] = jnp.zeros_like(dk_acc)
    dv_acc[...] = jnp.zeros_like(dv_acc)
    key_start = block * size
    lower, upper = bounds_ref[4, block], bounds_ref[5, block]

    def visit(query_block, masked):
        query_start = pl.multiple_of(query_block * size, size)
        rows = pl.ds(query_start, size)
        if masked:
            allowed = allowed_tile(
                key_start, query_start, low_ref[:, rows], high_ref[:, rows], size
            )
        for head in range(heads):
            group = head * HEAD_DIM // pair_width
            lanes = slice(group * pair_width, (group + 1) * pair_width)
            query, grad = qh_ref[head, rows, :], doh_ref[head, rows, :]
            scores = dot_f32(k_ref[:, lanes], query, NT)
            weights = jnp.exp(scores - lse_ref[head : head + 1, rows])
            if masked:
                weights = jnp.where(allowed, weights, 0.0)
            dv_acc[:, lanes] += dot_f32(weights.astype(jnp.bfloat16), grad, NN)
            d_weights = dot_f32(v_ref[:, lanes], grad, NT)
            d_scores = (weights * (d_weights - delta_ref[head, :, rows])).astype(jnp.bfloat16)
            dk_acc[:, lanes] += dot_f32(d_scores, query, NN)
            feats = slice(head * HEAD_DIM, (head + 1) * HEAD_DIM)
            dqt_ref[feats, rows] += dot_f32(kt_ref[feats, :], d_scores, NN)

    def step(query_block, carry):
        full = (key_start >= bounds_ref[1, query_block]) & (
            key_start + size <= bounds_ref[2, query_block]
        )
        pl.when(full)(lambda: visit(query_block, False))
        pl.when(jnp.logical_not(full))(lambda: visit(query_block, True))
        return carry

    lax.fori_loop(lower, upper, step, 0)
    dk_ref[...] = dk_acc[...].astype(jnp.bfloat16)
    dv_ref[...] = dv_acc[...].astype(jnp.bfloat16)

    @pl.when(block == blocks - 1)
    def _():
        def finish(index, carry):
            rows = pl.ds(pl.multiple_of(index * size, size), size)
            dq_ref[rows, :] = (dqt_ref[:, rows] * 0.125).T.astype(jnp.bfloat16)
            return carry

        lax.fori_loop(0, blocks, finish, 0)


def attend_backward(q, k, v, kt, d_ctx, ctx, lse, low, high, bounds):
    tokens, width = q.shape
    size = block_size_of(tokens)
    heads = width // HEAD_DIM
    pair_width = min(128, width)
    once = pl.Buffered(1)
    whole = pl.BlockSpec((tokens, width), lambda i, b: (0, 0), pipeline_mode=once)
    block = pl.BlockSpec((size, width), lambda i, b: (i, 0))
    row = pl.BlockSpec((1, tokens), lambda i, b: (0, 0), pipeline_mode=once)
    return pl.pallas_call(
        functools.partial(backward_body, size, heads, pair_width),
        name="attend_backward",
        out_shape=[jax.ShapeDtypeStruct((tokens, width), jnp.bfloat16)] * 3,
        grid_spec=pltpu.PrefetchScalarGridSpec(
            num_scalar_prefetch=1,
            grid=(tokens // size,),
            in_specs=[
                whole, block, block,
                pl.BlockSpec((width, size), lambda i, b: (0, i)),
                whole, whole,
                pl.BlockSpec((heads, tokens), lambda i, b: (0, 0), pipeline_mode=once),
                row, row,
            ],
            out_specs=[whole, block, block],
            scratch_shapes=[
                pltpu.VMEM((heads, tokens, pair_width), jnp.bfloat16),
                pltpu.VMEM((heads, tokens, pair_width), jnp.bfloat16),
                pltpu.VMEM((heads, 1, tokens), jnp.float32),
                pltpu.VMEM((width, tokens), jnp.float32),
                pltpu.VMEM((size, width), jnp.float32),
                pltpu.VMEM((size, width), jnp.float32),
            ],
        ),
        compiler_params=pltpu.CompilerParams(vmem_limit_bytes=48 << 20),
    )(bounds, q, k, v, kt, d_ctx, ctx, lse, low, high)


def key_bounds(seg_row, valid_row, size):
    tokens = seg_row.shape[0]
    ids = jnp.arange(8, dtype=jnp.int32)
    starts = jnp.sum((seg_row[None, :] < ids[:, None]).astype(jnp.int32), axis=1)
    ends = jnp.sum((seg_row[None, :] <= ids[:, None]).astype(jnp.int32), axis=1)
    valid_count = jnp.sum(valid_row)
    member = seg_row[None, :] == ids[:, None]
    low = jnp.sum(jnp.where(member, starts[:, None], 0), axis=0)
    end = jnp.sum(jnp.where(member, ends[:, None], 0), axis=0)
    high = jnp.minimum(end, valid_count)
    first_key = jnp.arange(0, tokens, size, dtype=jnp.int32)
    own = first_key // size
    live = first_key < valid_count
    seg_blocks = seg_row.reshape(-1, size)
    last_live = jnp.minimum(first_key + size, valid_count) - 1
    last_text = jnp.sum((starts[None, :] <= last_live[:, None]).astype(jnp.int32), axis=1) - 1
    last_end = jnp.sum(jnp.where(last_text[:, None] == ids[None, :], ends[None, :], 0), axis=1)
    low_blocks, high_blocks = low.reshape(-1, size), high.reshape(-1, size)
    query_from = jnp.where(live, low_blocks[:, 0] // size, own)
    query_to = jnp.where(live, jnp.maximum((last_end + size - 1) // size, own + 1), own + 1)
    bounds = jnp.stack(
        [low_blocks[:, 0], low_blocks[:, -1], high_blocks[:, 0], high_blocks[:, -1], query_from, query_to]
    )
    return low[None, :], high[None, :], bounds


from jax.sharding import PartitionSpec as P

EPSILON = 1e-05
EVERY = ("tensor", "batch")


def inner_first(left, right):
    return dot_f32(left, right, (((0,), (0,)), ((), ())))


def inner_last(left, right):
    return dot_f32(left, right, NT)


def gelu_exact(value):
    return 0.5 * value * (1.0 + lax.erf(value * (1.0 / math.sqrt(2.0))))


def norm_stats(value):
    mean_value = jnp.mean(value, axis=1, keepdims=True)
    spread = jnp.mean(value * value, axis=1, keepdims=True) - mean_value * mean_value
    return mean_value, lax.rsqrt(spread + EPSILON)


def norm_backward(d_scaled, normed, scale):
    return scale * (
        d_scaled
        - jnp.mean(d_scaled, axis=1, keepdims=True)
        - normed * jnp.mean(d_scaled * normed, axis=1, keepdims=True)
    )


def batch_piece(weight):
    rows = weight.shape[0] // lax.axis_size("batch")
    return lax.dynamic_slice_in_dim(weight, lax.axis_index("batch") * rows, rows, 0)


def gather_weight(weight):
    return lax.all_gather(batch_piece(weight), EVERY, axis=0, tiled=True)


def heads_to_tokens(value):
    return lax.all_to_all(value, "tensor", split_axis=0, concat_axis=1, tiled=True)


def tokens_to_heads(value):
    return lax.all_to_all(value, "tensor", split_axis=1, concat_axis=0, tiled=True)


def reduce_weight(grad):
    part = lax.psum_scatter(grad.astype(jnp.bfloat16), "batch", scatter_dimension=0, tiled=True)
    return part


def local(
    inputs,
    segments,
    valid,
    w_query,
    b_query,
    w_key,
    w_value,
    b_value,
    w_out,
    b_out,
    gain_one,
    shift_one,
    w_up,
    b_up,
    w_down,
    b_down,
    gain_two,
    shift_two,
    lex_weight,
    lex_bias,
    cotangent,
):
    row_count, seq_len, full_width = inputs.shape
    token_count = row_count * seq_len
    shards = lax.axis_size("tensor")
    members = lax.axis_size("batch")
    me = lax.axis_index("tensor")
    slice_width = full_width // shards
    own_count = token_count // shards
    flat = inputs.reshape(token_count, full_width)
    size = block_size_of(seq_len)

    out_full = gather_weight(w_out)
    up_full = gather_weight(w_up.T)
    down_full = gather_weight(w_down)
    small = jnp.concatenate(
        [b_out, gain_one, shift_one, b_down, gain_two, shift_two, lex_weight, b_up]
    )
    small_all = lax.all_gather(small, "tensor", axis=0).astype(jnp.float32)
    vectors = [
        small_all[:, i * slice_width : (i + 1) * slice_width].reshape(1, full_width)
        for i in range(7)
    ]
    b_out_v, gain_one_v, shift_one_v, b_down_v, gain_two_v, shift_two_v, lex_v = vectors
    b_up_v = small_all[:, 7 * slice_width :].reshape(1, -1)

    queries = (jnp.dot(flat, w_query, preferred_element_type=jnp.float32) + b_query).astype(
        jnp.bfloat16
    )
    key_rows = jnp.dot(flat, w_key, preferred_element_type=jnp.float32).astype(jnp.bfloat16)
    value_rows = (jnp.dot(flat, w_value, preferred_element_type=jnp.float32) + b_value).astype(
        jnp.bfloat16
    )
    d_final = heads_to_tokens(cotangent.reshape(token_count, slice_width)).astype(jnp.float32)
    rows = []
    for row in range(row_count):
        span = slice(row * seq_len, (row + 1) * seq_len)
        low, high, bounds = key_bounds(segments[row], valid[row], size)
        row_q, row_k, row_v = queries[span], key_rows[span], value_rows[span]
        row_ctx, row_lse = attend_forward(row_q, row_k, row_v.T, low, high, bounds)
        rows.append((row_q, row_k, row_v, row_ctx, row_lse, low, high, bounds))
    context = jnp.concatenate([item[3] for item in rows], axis=0)

    token_ctx = heads_to_tokens(context)
    own_input = lax.dynamic_slice_in_dim(flat, me * own_count, own_count, 0).astype(jnp.float32)
    first_res = own_input + jnp.dot(token_ctx, out_full, preferred_element_type=jnp.float32) + b_out_v
    mean_one, scale_one = norm_stats(first_res)
    normed_one = (first_res - mean_one) * scale_one
    first_out = normed_one * gain_one_v + shift_one_v
    first_low = first_out.astype(jnp.bfloat16)
    pre_up = inner_last(first_low, up_full) + b_up_v
    hidden = gelu_exact(pre_up).astype(jnp.bfloat16)
    second_res = first_out + jnp.dot(hidden, down_full, preferred_element_type=jnp.float32) + b_down_v
    mean_two, scale_two = norm_stats(second_res)
    normed_two = (second_res - mean_two) * scale_two
    final_out = normed_two * gain_two_v + shift_two_v
    output = tokens_to_heads(final_out.astype(jnp.bfloat16))
    lex_pre = jnp.sum(final_out * lex_v, axis=1) + lex_bias[0].astype(jnp.float32)
    valid_float = lax.dynamic_slice_in_dim(
        valid.reshape(token_count), me * own_count, own_count, 0
    ).astype(jnp.float32)
    lex_totals = jnp.stack(
        [
            jnp.sum(valid_float),
            jnp.sum(jnp.maximum(lex_pre, 0.0) * valid_float),
            jnp.sum(jnp.where(lex_pre > 0.0, valid_float, 0.0)),
        ]
    )

    grad_gain_two = jnp.sum(d_final * normed_two, axis=0)
    grad_shift_two = jnp.sum(d_final, axis=0)
    d_second = norm_backward(d_final * gain_two_v, normed_two, scale_two)
    grad_b_down = jnp.sum(d_second, axis=0)
    d_ffn_low = d_second.astype(jnp.bfloat16)
    d_hidden = inner_last(d_ffn_low, down_full)
    _, gelu_back = jax.vjp(gelu_exact, pre_up)
    d_pre_up = gelu_back(d_hidden)[0].astype(jnp.bfloat16)
    grad_b_up = jnp.sum(d_pre_up, axis=0, dtype=jnp.float32)
    d_first = d_second + jnp.dot(d_pre_up, up_full, preferred_element_type=jnp.float32)
    grad_gain_one = jnp.sum(d_first * normed_one, axis=0)
    grad_shift_one = jnp.sum(d_first, axis=0)
    d_first_res = norm_backward(d_first * gain_one_v, normed_one, scale_one)
    grad_b_out = jnp.sum(d_first_res, axis=0)
    d_attn_low = d_first_res.astype(jnp.bfloat16)
    d_context = tokens_to_heads(inner_last(d_attn_low, out_full).astype(jnp.bfloat16))

    weight_grads = []
    for left, right in ((hidden, d_ffn_low), (d_pre_up, first_low), (token_ctx, d_attn_low)):
        grad = inner_first(left, right)
        grad = grad.reshape(shards, members, -1, full_width).transpose(1, 0, 2, 3)
        part = lax.psum_scatter(
            grad.astype(jnp.bfloat16), "batch", scatter_dimension=0, tiled=True
        )[0]
        part = lax.psum_scatter(part, "tensor", scatter_dimension=0, tiled=True)[0]
        weight_grads.append(
            lax.all_gather(part, "batch", axis=0, tiled=True).astype(jnp.float32)
        )
    grad_w_down, grad_w_up_t, grad_w_out = weight_grads
    token_sums = jnp.concatenate(
        [
            item.reshape(shards, -1)
            for item in (
                grad_b_out,
                grad_gain_one,
                grad_shift_one,
                grad_b_down,
                grad_gain_two,
                grad_shift_two,
                grad_b_up,
                jnp.broadcast_to(lex_totals, (shards, 3)),
            )
        ],
        axis=1,
    )
    own_sums = lax.dynamic_index_in_dim(lax.psum(token_sums, EVERY), me, 0, False)
    sums = [own_sums[i * slice_width : (i + 1) * slice_width] for i in range(6)]
    sum_b_up = own_sums[6 * slice_width : -3]
    totals_all = own_sums[-3:]
    lex_stats = jnp.stack([totals_all[1] / totals_all[0], totals_all[2] / totals_all[0]])

    grads = []
    for row in range(row_count):
        row_q, row_k, row_v, row_ctx, row_lse, low, high, bounds = rows[row]
        grads.append(
            attend_backward(
                row_q, row_k, row_v, row_k.T,
                d_context[row * seq_len : (row + 1) * seq_len],
                row_ctx, row_lse, low, high, bounds,
            )
        )
    d_queries, d_keys, d_values = (
        jnp.concatenate([item[i] for item in grads], axis=0) for i in range(3)
    )
    d_input_term = (
        inner_last(d_queries, w_query) + inner_last(d_keys, w_key) + inner_last(d_values, w_value)
    )
    own_term = lax.dynamic_slice_in_dim(d_input_term, me * own_count, own_count, 0) + d_first_res
    d_input_term = lax.dynamic_update_slice_in_dim(
        d_input_term.astype(jnp.bfloat16), own_term.astype(jnp.bfloat16), me * own_count, 0
    )
    grad_inputs = lax.psum_scatter(d_input_term, "tensor", scatter_dimension=1, tiled=True)
    head_sums = [
        inner_first(flat, d_queries),
        inner_first(flat, d_keys),
        inner_first(flat, d_values),
        jnp.sum(d_queries, axis=0, dtype=jnp.float32),
        jnp.sum(d_values, axis=0, dtype=jnp.float32),
    ]
    head_sums = [
        lax.psum(item.astype(jnp.bfloat16), "batch").astype(jnp.float32) for item in head_sums
    ]
    out_shape = (row_count, seq_len, slice_width)
    return (
        output.reshape(out_shape),
        grad_inputs.reshape(out_shape),
        head_sums[0],
        head_sums[3],
        head_sums[1],
        head_sums[2],
        head_sums[4],
        grad_w_out,
        sums[0],
        sums[1],
        sums[2],
        grad_w_up_t.T,
        sum_b_up,
        grad_w_down,
        sums[3],
        sums[4],
        sums[5],
        lex_stats,
    )


def solution(mesh):
    in_specs = (
        P("batch", None, None),
        P("batch", None),
        P("batch", None),
        P(None, "tensor"),
        P("tensor"),
        P(None, "tensor"),
        P(None, "tensor"),
        P("tensor"),
        P("tensor", None),
        P("tensor"),
        P("tensor"),
        P("tensor"),
        P(None, "tensor"),
        P("tensor"),
        P("tensor", None),
        P("tensor"),
        P("tensor"),
        P("tensor"),
        P("tensor"),
        P(),
        P("batch", None, "tensor"),
    )
    out_specs = (
        P("batch", None, "tensor"),
        P("batch", None, "tensor"),
        P(None, "tensor"),
        P("tensor"),
        P(None, "tensor"),
        P(None, "tensor"),
        P("tensor"),
        P("tensor", None),
        P("tensor"),
        P("tensor"),
        P("tensor"),
        P(None, "tensor"),
        P("tensor"),
        P("tensor", None),
        P("tensor"),
        P("tensor"),
        P("tensor"),
        P(),
    )
    return jax.shard_map(local, mesh=mesh, in_specs=in_specs, out_specs=out_specs, check_vma=False)
```

time: 2710 us -> 1050 us (0.39)
  matrix products: 1030 us -> 195 us
  waiting for transfers between devices: 1000 us -> 373 us
  other arithmetic: 458 us -> 42 us
  Pallas kernels: 0 us -> 151 us
  blocking collectives: 84 us -> 180 us
  loops' own time: 27.4 us -> 0 us
    dot_general x71 -> x15, matrix products: 1010 us -> 175 us  [the longest x12 133 us: dot_f32(): lax.dot_general(left, right, dims, preferred_element_type=jnp.float32)]
    all_gather x4 -> x5, waiting for transfers between devices: 540 us -> 71 us  [the longest x3 71 us: gather_weight(): return lax.all_gather(batch_piece(weight), EVERY, axis=0, tiled=True)]
    reduce_scatter x3 -> x6, waiting for transfers between devices: 411 us -> 101 us  [the longest x3 55.3 us: local(): part = lax.psum_scatter(part, 'tensor', scatter_dimension=0, tiled=True)[0]]
    convert_element_type x31 -> x4, other arithmetic: 250 us -> 6.28 us  [the longest x2 5.15 us: local(): lax.all_gather(part, 'batch', axis=0, tiled=True).astype(jnp.float32)]
    pallas_call x0 -> x2, Pallas kernels: none -> 151 us  [the longest x1 81.7 us: attend_backward(): pl.pallas_call(functools.partial(backward_body, size, heads, pair_width),...]
    reduce_sum x14 -> x11, other arithmetic: 136 us -> 9.85 us  [the longest x1 3.88 us: local(): grad_b_down = jnp.sum(d_second, axis=0)]
    psum x1, waiting for transfers between devices: 34.7 us -> 157 us  [local(): lax.psum(item.astype(jnp.bfloat16), 'batch').astype(jnp.float32)]
    all_gather x0 -> x2, blocking collectives: none -> 80.6 us  [the longest x1 71.4 us: local(): small_all = lax.all_gather(small, 'tensor', axis=0).astype(jnp.float32)]
  transfers between devices with their start and end apart: 9 -> 16, of which waited for: 9 -> 6; matrix products, arithmetic and copies ran while one was open for 4% -> 21% of each run, Pallas kernels for 0% -> 14%
where the time goes in v1:
time: 1050 us
  waiting for transfers between devices  373 us (36%)
  matrix products  195 us (19%)
  blocking collectives  180 us (17%)
  Pallas kernels  151 us (14%)
  local copies, waits for them, and re-layouts  68 us (6%)
  other arithmetic  42 us (4%)
  starting transfers between devices  20.7 us (2%)
  between operations  18.4 us (2%)
    psum x1, waiting for transfers between devices, local(): lax.psum(item.astype(jnp.bfloat16), 'batch').astype(jnp.float32)  157 us
    dot_general x12, matrix products, dot_f32(): lax.dot_general(left, right, dims, preferred_element_type=jnp.float32)  133 us
    psum x1, blocking collectives, local(): lax.psum(token_sums, EVERY)  86.2 us
    pallas_call x1, Pallas kernels, attend_backward(): pl.pallas_call(functools.partial(backward_body, size, heads, pair_width),...  81.7 us
    all_gather x1, blocking collectives, local(): small_all = lax.all_gather(small, 'tensor', axis=0).astype(jnp.float32)  71.4 us
    all_gather x3, waiting for transfers between devices, gather_weight(): return lax.all_gather(batch_piece(weight), EVERY, axis=0, tiled=True)  71 us
    pallas_call x1, Pallas kernels, attend_forward(): pl.pallas_call(functools.partial(forward_body, first, size, heads, pair_w...  69.2 us
    reduce_scatter x3, waiting for transfers between devices, local(): part = lax.psum_scatter(part, 'tensor', scatter_dimension=0, tiled=True)[0]  55.3 us
  transfers between devices with their start and end apart: 16, of which 6 were waited for; matrix products, arithmetic and copies ran while one was open for 21% of the time, Pallas kernels for 14%

profile of v1, /device:TPU:0, one launch (start us, length us, event | category | flops | bytes accessed | tf_op | source)
XLA Modules:
  0.0 1048.7 jit_solution(18011186325333521098)
XLA Ops:
  15.6 6.3 all-to-all-start.2
  23.7 7.1 fusion.18
  34.2 7.8 fusion.21.v_ref
  48.1 5.9 fusion.24.q_ref
  54.0 69.2 %attend_forward.1 = (bf16[4096,256]{1,0:T(8,128)(2,1)S(1)}, f32[4,4096]{1,0:T(4,128)S(1)}) custom-call(s32[6,16]{1,0:T(8,128)S(1)} %stack.26.bounds_ref, bf16[4096,256]{1,0:T(8,128)(2,1)S(1)} %fusion.24.q_ref, bf16[4096,256]{1,0:T(8,128)(2,1)S(1)} %copy.120.k_ref, bf16[256,4096]{1,0:T(8,128)(2,1)S(1)} %copy-done.6, s32[1,4096]{1,0:T(1,128)S(1)} %bitcast.213, ...), custom_call_target="tpu_custom_call" | custom-call | tf_op jit(solution)/shard_map/attend_forward/pallas_call | solution.py:106
  140.1 71.4 %all-gather.4 = bf16[4,1,2816]{2,1,0:T(2,128)(2,1)S(1)} all-gather(bf16[1,1,2816]{2,1,0:T(2,128)(2,1)S(1)} %reshape.433), channel_id=2, replica_groups=mesh['batch'=8,'tensor'=4] {'tensor'}, dimensions={0}, use_global_device_ids=true | all-gather | bytes 28160 | tf_op jit(solution)/shard_map/all_gather | solution.py:370
  214.9 7.7 fusion.73
  222.7 20.3 %multiply_convert_fusion = (bf16[1024,4096]{1,0:T(8,128)(2,1)}, f32[1024,4096]{1,0:T(8,128)}) fusion(f32[4096]{0:T(1024)S(1)} %bitcast.247, bf16[4096,1024]{0,1:T(8,128)(2,1)} %all-gather.13.cloned.1.call-done, f32[1024,1024]{0,1:T(8,128)} %get-tuple-element.173, f32[1024]{0:T(1024)S(1)} %bitcast.252, f32[1024]{0:T(1024)S(1)} %bitcast.240, ...), kind=kOutput, calls=%fused_computation.3 | convolution fusion | flops 8620343296 | bytes 37781504 | tf_op jit(solution)/shard_map/dot_general | solution.py:15
  243.0 71.0 %all-gather.15.cloned.1.call-done = bf16[4096,1024]{1,0:T(8,128)(2,1)} async-done(((bf16[128,1024]{1,0:T(8,128)(2,1)}), bf16[4096,1024]{1,0:T(8,128)(2,1)}) %all-gather.15.cloned.1.call-update) | async-done | bytes 8388624 | tf_op jit(solution)/shard_map/all_gather | solution.py:315
  314.1 16.5 %fusion.72 = (f32[1024]{0:T(1024)S(1)}, f32[1024]{0:T(1024)S(1)}, f32[1024,1024]{0,1:T(8,128)}) fusion(f32[1024]{0:T(1024)S(1)} %bitcast.255, bf16[1024,4096]{1,0:T(8,128)(2,1)} %get-tuple-element.174, bf16[4096,1024]{1,0:T(8,128)(2,1)} %all-gather.15.cloned.1.call-done, f32[1024]{0:T(1024)S(1)} %bitcast.253, f32[1024]{0:T(1024)S(1)} %bitcast.241, ...), kind=kOutput, calls=%fused_computation.145 | convolution fusion | flops 8599369728 | bytes 25194496 | tf_op jit(solution)/shard_map/dot_general | solution.py:404
  330.6 6.3 fusion.36
  340.9 21.0 %convert_reduce_fusion = (f32[4096]{0:T(1024)S(1)}, bf16[1024,4096]{1,0:T(8,128)(2,1)}) fusion(bf16[4096,1024]{1,0:T(8,128)(2,1)S(1)} %copy-done.37, f32[1024,1024]{0,1:T(8,128)S(1)} %get-tuple-element.148, f32[1024,4096]{1,0:T(8,128)} %get-tuple-element.175, f32[4096]{0:T(1024)S(1)} %bitcast.248), kind=kOutput, calls=%fused_computation | convolution fusion | flops 8658087936 | bytes 37781504 | tf_op jit(solution)/shard_map/dot_general | solution.py:15
  361.9 15.4 %convolution_convert_fusion.1 = bf16[4096,1024]{1,0:T(8,128)(2,1)} fusion(bf16[1024,4096]{1,0:T(8,128)(2,1)} %get-tuple-element.181, f32[1024,1024]{0,1:T(8,128)S(1)} %copy-done.11, f32[1024]{0:T(1024)S(1)} %bitcast.254, f32[1024]{0:T(1024)S(1)} %bitcast.242, f32[1024]{0:T(1024)S(1)} %get-tuple-element.172, f32[1024]{0:T(1024)S(1)} %get-tuple-element.171), kind=kOutput, calls=%fused_computation.19 | convolution fusion | flops 8599371776 | bytes 20987904 | tf_op jit(solution)/shard_map/dot_general | solution.py:15
  377.3 11.5 %copy.132 = bf16[4,8,128,1024]{2,3,0,1:T(8,128)(2,1)} copy(bf16[4,8,128,1024]{3,2,1,0:T(8,128)(2,1)} %bitcast.221) | data formatting | bytes 16777216 | tf_op jit(solution)/shard_map/convert_element_type | solution.py:443
  388.9 15.6 %convolution_convert_fusion = bf16[4096,1024]{1,0:T(8,128)(2,1)} fusion(bf16[1024,4096]{1,0:T(8,128)(2,1)} %get-tuple-element.174, f32[1024,1024]{0,1:T(8,128)} %copy-done.13), kind=kOutput, calls=%fused_computation.18 | convolution fusion | flops 8595177472 | bytes 20971520 | tf_op jit(solution)/shard_map/dot_general | solution.py:15
  404.6 8.3 copy.160
  412.9 17.3 %multiply_reduce_fusion.1 = (f32[1024]{0:T(1024)S(1)}, f32[1024]{0:T(1024)S(1)}, f32[1024]{0:T(1024)S(1)}, f32[1024]{0:T(1024)S(1)}, f32[1024,1024]{0,1:T(8,128)S(1)}) fusion(f32[1024,1024]{0,1:T(8,128)} %get-tuple-element.173, f32[1024]{0:T(1024)S(1)} %get-tuple-element.172, f32[1024]{0:T(1024)S(1)} %get-tuple-element.171, f32[1024]{0:T(1024)S(1)} %bitcast.243, ...), kind=kOutput, calls=%fused_computation.41 | convolution fusion | flops 8600416256 | bytes 29388800 | tf_op jit(solution)/shard_map/dot_general | solution.py:430
  440.8 6.5 convert_bitcast_fusion.2
  447.2 42.2 %all-to-all-done.3 = bf16[1024,4,256]{2,0,1:T(8,128)(2,1)S(1)} async-done(((bf16[1024,4,256]{2,0,1:T(8,128)(2,1)}), bf16[1024,4,256]{2,0,1:T(8,128)(2,1)S(1)}, u32[]{:S(2)}, u32[]{:S(2)}) %all-to-all-start.3) | async-done | bytes 2097184 | tf_op jit(solution)/shard_map/all_to_all | solution.py:323
  490.8 81.7 %attend_backward.1 = (bf16[4096,256]{1,0:T(8,128)(2,1)S(1)}, bf16[4096,256]{1,0:T(8,128)(2,1)S(1)}, bf16[4096,256]{1,0:T(8,128)(2,1)}) custom-call(s32[6,16]{1,0:T(8,128)S(1)} %stack.26.bounds_ref, bf16[4096,256]{1,0:T(8,128)(2,1)} %copy-done.7, bf16[4096,256]{1,0:T(8,128)(2,1)} %copy-done.4, bf16[4096,256]{1,0:T(8,128)(2,1)} %fusion.21.v_ref, ...), custom_call_target="tpu_custom_call" | custom-call | tf_op jit(solution)/shard_map/attend_backward/pallas_call | solution.py:223
  572.5 8.0 fusion.53
  589.0 157.2 %all-reduce.5.cloned.1.call-done = (bf16[1024,256]{0,1:T(8,128)(2,1)}, bf16[1024,256]{0,1:T(8,128)(2,1)}, bf16[1024,256]{0,1:T(8,128)(2,1)}, bf16[8,4,32,1024]{3,2,0,1:T(8,128)(2,1)}) async-done(((bf16[1024,256]{0,1:T(8,128)(2,1)}, bf16[1024,256]{0,1:T(8,128)(2,1)}, bf16[1024,256]{0,1:T(8,128)(2,1)}, bf16[8,4,32,1024]{3,2,0,1:T(8,128)(2,1)}), (bf16[1024,256]{0,1:T(8,128)(2,1)}, bf16[1024,256]{0,1:T(8,128)(2,1)}, ...) | async-done | bytes 3670032 | tf_op jit(solution)/shard_map/psum | solution.py:501
  748.6 27.3 %reduce-scatter.16.cloned.1.call-done = bf16[1,128,1024]{1,2,0:T(8,128)(2,1)} async-done(((bf16[4,128,1024]{1,2,0:T(8,128)(2,1)}), bf16[1,128,1024]{1,2,0:T(8,128)(2,1)}) %reduce-scatter.16.cloned.1.call-update) | async-done | bytes 262160 | tf_op jit(solution)/shard_map/reduce_scatter | solution.py:445
  775.9 28.0 %reduce-scatter.20.cloned.1.call-done = bf16[1,128,1024]{2,1,0:T(8,128)(2,1)} async-done(((bf16[4,128,1024]{2,1,0:T(8,128)(2,1)}), bf16[1,128,1024]{2,1,0:T(8,128)(2,1)}) %reduce-scatter.20.cloned.1.call-update) | async-done | bytes 262160 | tf_op jit(solution)/shard_map/reduce_scatter | solution.py:445
  804.2 8.1 fusion.82
  812.3 8.1 fusion.83
  820.4 21.5 %fusion.81 = (bf16[4096,1024]{0,1:T(8,128)(2,1)}, f32[4096,1024]{0,1:T(8,128)}) fusion(bf16[4096,256]{1,0:T(8,128)(2,1)} %get-tuple-element.27, bf16[1024,256]{1,0:T(8,128)(2,1)S(1)} %copy-done.15, f32[4096,1024]{0,1:T(8,128)} %fusion.82, f32[4096,1024]{0,1:T(8,128)} %fusion.83), kind=kOutput, calls=%fused_computation.153 | convolution fusion | flops 2160066560 | bytes 61341696 | tf_op jit(solution)/shard_map/dot_general | solution.py:15
  841.9 6.0 fusion.39
  857.1 86.2 %psum.47 = f32[4,2563]{1,0:T(4,128)S(1)} all-reduce(f32[4,2563]{1,0:T(4,128)S(1)} %constant_dynamic-update-slice_fusion), channel_id=1, replica_groups=mesh['batch'=8,'tensor'=4] {'tensor','batch'}, use_global_device_ids=true, to_apply=%region_36.37 | all-reduce | flops 10252 | bytes 82016 | tf_op jit(solution)/shard_map/psum | solution.py:466
  951.3 13.6 %all-reduce.1 = (bf16[256]{0:T(256)(128)(2,1)S(1)}, bf16[256]{0:T(256)(128)(2,1)S(1)}) all-reduce(bf16[256]{0:T(256)(128)(2,1)S(1)} %reduce_sum.273, bf16[256]{0:T(256)(128)(2,1)S(1)} %reduce_sum.274), channel_id=1, replica_groups=mesh['batch'=8,'tensor'=4] {'batch'}, use_global_device_ids=true, to_apply=%region_18.19 | all-reduce | flops 512 | bytes 2048 | tf_op jit(solution)/shard_map/psum | solution.py:501
  973.5 9.2 all-gather.1
  992.1 45.6 %reduce-scatter.10.cloned.1.call-done = bf16[4096,256]{0,1:T(8,128)(2,1)} async-done(((bf16[4096,1024]{0,1:T(8,128)(2,1)}), bf16[4096,256]{0,1:T(8,128)(2,1)}) %reduce-scatter.10.cloned.1.call-update) | async-done | bytes 2097168 | tf_op jit(solution)/shard_map/reduce_scatter | solution.py:492
  (221 shorter events, 102.4 us)
Async XLA Ops:
  7.2 207.7 %all-gather.11.cloned.1.call-start = ((), (), s32[]{:S(2)}) async-start(), calls=%async_computation.10 | async-start | bytes 2162688 | tf_op jit(solution)/shard_map/all_gather | solution.py:315
  8.9 213.8 %all-gather.13.cloned.1.call-start = ((), (), s32[]{:S(2)}) async-start(), calls=%async_computation.11 | async-start | bytes 8650752 | tf_op jit(solution)/shard_map/all_gather | solution.py:315
  9.8 304.3 %all-gather.15.cloned.1.call-start = ((), (), s32[]{:S(2)}) async-start(), calls=%async_computation.12 | async-start | bytes 8650752 | tf_op jit(solution)/shard_map/all_gather | solution.py:315
  11.5 10.4 copy-start.23
  11.5 10.9 %copy-start.24 = (s32[1,4096]{1,0:T(1,128)S(1)}, s32[1,4096]{1,0:T(1,128)}, u32[]{:S(2)}) copy-start(s32[1,4096]{1,0:T(1,128)} %param.23) | copy-start | bytes 49156
  11.5 12.2 %copy-start.18 = (bf16[1024,256]{1,0:T(8,128)(2,1)S(1)}, bf16[1024,256]{1,0:T(8,128)(2,1)}, u32[]{:S(2)}) copy-start(bf16[1024,256]{1,0:T(8,128)(2,1)} %param.26) | copy-start | bytes 1572868
  15.6 113.0 %all-to-all-start.2 = ((bf16[4,1024,256]{1,2,0:T(8,128)(2,1)}), bf16[4,1024,256]{1,2,0:T(8,128)(2,1)}, u32[]{:S(2)}, u32[]{:S(2)}) async-start(bf16[4,1024,256]{1,2,0:T(8,128)(2,1)} %copy.124), calls=%async_computation.2 | async-start | bytes 4194304 | tf_op jit(solution)/shard_map/all_to_all | solution.py:319
  34.2 19.8 %copy-start.4 = (bf16[4096,256]{1,0:T(8,128)(2,1)}, bf16[4096,256]{1,0:T(8,128)(2,1)S(1)}, u32[]{:S(2)}) copy-start(bf16[4096,256]{1,0:T(8,128)(2,1)S(1)} %copy.120.k_ref) | copy-start | bytes 6291460
  54.0 69.3 %copy-start.7 = (bf16[4096,256]{1,0:T(8,128)(2,1)}, bf16[4096,256]{1,0:T(8,128)(2,1)S(1)}, u32[]{:S(2)}) copy-start(bf16[4096,256]{1,0:T(8,128)(2,1)S(1)} %fusion.24.q_ref) | copy-start | bytes 6291460
  128.5 86.4 %all-to-all-start = ((bf16[4,1024,256]{1,2,0:T(8,128)(2,1)}), bf16[4,1024,256]{1,2,0:T(8,128)(2,1)}, u32[]{:S(2)}, u32[]{:S(2)}) async-start(bf16[4,1024,256]{1,2,0:T(8,128)(2,1)} %copy.122), calls=%async_computation | async-start | bytes 4194304 | tf_op jit(solution)/shard_map/all_to_all | solution.py:319
  133.6 453.3 %reduce-scatter.14.cloned.1.call-start = ((), (), s32[]{:S(2)}) async-start(), calls=%async_computation.15 | async-start | bytes 9437184 | tf_op jit(solution)/shard_map/reduce_scatter | solution.py:442
  340.8 21.1 %copy-start.13 = (f32[1024,1024]{0,1:T(8,128)}, f32[1024,1024]{0,1:T(8,128)S(1)}, u32[]{:S(2)}) copy-start(f32[1024,1024]{0,1:T(8,128)S(1)} %get-tuple-element.148) | copy-start | bytes 12582916
  340.9 21.0 %copy-start.11 = (f32[1024,1024]{0,1:T(8,128)S(1)}, f32[1024,1024]{0,1:T(8,128)}, u32[]{:S(2)}) copy-start(f32[1024,1024]{0,1:T(8,128)} %get-tuple-element.173) | copy-start | bytes 12582916
  388.9 198.7 %reduce-scatter.18.cloned.1.call-start = ((), (), s32[]{:S(2)}) async-start(), calls=%async_computation.17 | async-start | bytes 9437184 | tf_op jit(solution)/shard_map/reduce_scatter | solution.py:442
  412.8 17.3 %copy-start.12 = (f32[1024,1024]{0,1:T(8,128)S(1)}, f32[1024,1024]{0,1:T(8,128)}, u32[]{:S(2)}) copy-start(f32[1024,1024]{0,1:T(8,128)} %get-tuple-element.173) | copy-start | bytes 12582916
  436.8 52.7 %all-to-all-start.3 = ((bf16[1024,4,256]{2,0,1:T(8,128)(2,1)}), bf16[1024,4,256]{2,0,1:T(8,128)(2,1)S(1)}, u32[]{:S(2)}, u32[]{:S(2)}) async-start(bf16[1024,4,256]{2,0,1:T(8,128)(2,1)} %copy.126), calls=%async_computation.3 | async-start | bytes 4194304 | tf_op jit(solution)/shard_map/all_to_all | solution.py:323
  440.8 305.4 %all-reduce.5.cloned.1.call-start = ((), (), s32[]{:S(2)}) async-start(), calls=%async_computation.21 | async-start | bytes 7340032 | tf_op jit(solution)/shard_map/psum | solution.py:501
  490.8 89.7 %slice-start = ((s8[8388608]{0:T(1024)(128)(4,1)}), s8[4194304]{0:T(1024)(128)(4,1)S(1)}, s32[]{:S(2)}) async-start(s8[8388608]{0:T(1024)(128)(4,1)} %bitcast.217), calls=%async_computation.22 | async-start | bytes 8388608
  586.8 217.4 %copy-start.17 = (bf16[1024,256]{1,0:T(8,128)(2,1)S(1)}, bf16[1024,256]{1,0:T(8,128)(2,1)}, u32[]{:S(2)}) copy-start(bf16[1024,256]{1,0:T(8,128)(2,1)} %param.24) | copy-start | bytes 1572868
  586.8 189.0 %reduce-scatter.16.cloned.1.call-start = ((), (), s32[]{:S(2)}) async-start(), calls=%async_computation.16 | async-start | bytes 1310720 | tf_op jit(solution)/shard_map/reduce_scatter | solution.py:445
  587.6 216.4 %reduce-scatter.20.cloned.1.call-start = ((), (), s32[]{:S(2)}) async-start(), calls=%async_computation.18 | async-start | bytes 1310720 | tf_op jit(solution)/shard_map/reduce_scatter | solution.py:445
  588.3 385.2 %reduce-scatter.12.cloned.1.call-start = ((), (), s32[]{:S(2)}) async-start(), calls=%async_computation.14 | async-start | bytes 327680 | tf_op jit(solution)/shard_map/reduce_scatter | solution.py:445
  748.5 235.2 %all-gather.17.cloned.1.call-start = ((), (), s32[]{:S(2)}) async-start(), calls=%async_computation.19 | async-start | bytes 2359296 | tf_op jit(solution)/shard_map/all_gather | solution.py:447
  775.9 212.1 %all-gather.19.cloned.1.call-start = ((), (), s32[]{:S(2)}) async-start(), calls=%async_computation.20 | async-start | bytes 2359296 | tf_op jit(solution)/shard_map/all_gather | solution.py:447
  804.0 8.3 copy-start.19
  804.0 233.6 %reduce-scatter.10.cloned.1.call-start = ((), (), s32[]{:S(2)}) async-start(), calls=%async_computation.13 | async-start | bytes 10485760 | tf_op jit(solution)/shard_map/reduce_scatter | solution.py:492
  847.9 9.2 copy-start.25
  847.9 118.2 %all-to-all-start.1 = ((bf16[1024,4,256]{0,2,1:T(8,128)(2,1)}), bf16[1024,4,256]{0,2,1:T(8,128)(2,1)}, u32[]{:S(2)}, u32[]{:S(2)}) async-start(bf16[1024,4,256]{0,2,1:T(8,128)(2,1)} %bitcast.223), calls=%async_computation.1 | async-start | bytes 4194304 | tf_op jit(solution)/shard_map/all_to_all | solution.py:323
  948.5 21.5 %copy-start.22 = (bf16[1024,256]{0,1:T(8,128)(2,1)S(1)}, bf16[1024,256]{0,1:T(8,128)(2,1)}, u32[]{:S(2)}) copy-start(bf16[1024,256]{0,1:T(8,128)(2,1)} %get-tuple-element.141) | copy-start | bytes 1572868
  949.1 22.1 %copy-start.21 = (bf16[1024,256]{0,1:T(8,128)(2,1)S(1)}, bf16[1024,256]{0,1:T(8,128)(2,1)}, u32[]{:S(2)}) copy-start(bf16[1024,256]{0,1:T(8,128)(2,1)} %get-tuple-element.142) | copy-start | bytes 1572868
  951.3 21.1 %copy-start.20 = (bf16[1024,256]{0,1:T(8,128)(2,1)S(1)}, bf16[1024,256]{0,1:T(8,128)(2,1)}, u32[]{:S(2)}) copy-start(bf16[1024,256]{0,1:T(8,128)(2,1)} %get-tuple-element.143) | copy-start | bytes 1572868
  983.8 57.9 %copy-start.1 = (bf16[1024,1024]{1,0:T(8,128)(2,1)S(1)}, bf16[1024,1024]{1,0:T(8,128)(2,1)}, u32[]{:S(2)}) copy-start(bf16[1024,1024]{1,0:T(8,128)(2,1)} %param.33) | copy-start | bytes 6291460
  (28 other events, 136.7 us)
Sparse Core Ops, SparseCore 0:
  11.4 75.5 all-gather.10
  90.5 121.3 all-gather.12
  215.3 98.6 all-gather.14
  389.0 70.1 reduce-scatter.13
  462.5 71.4 reduce-scatter.17
  586.9 159.2 all-reduce.4
  748.5 27.3 reduce-scatter.15
  778.1 25.7 reduce-scatter.19
  806.8 18.4 reduce-scatter.11
  827.0 26.3 all-gather.16
  855.3 27.9 all-gather.18
  885.5 152.1 reduce-scatter.9
